TPU v7x, 128 devices: a whole 4x4x4 slice. The times are simulated.
128 devices in a mesh: seq: 16 (over z_hi, y, core), head: 8 (over x, z_lo).
Axes of the slice: x: 4, y: 4, z: 4 (z_hi: 2, z_lo: 2; z = z_hi * 2 + z_lo), core: 2. Of those that a mesh axis runs over, the one named last changes fastest.
Arguments:
- latent: bfloat16 [16, 1024, 2048], P('seq', None, 'head'), may hold values from -6 to 6
- modulation: float32 [9, 2048], replicated, may hold values from -3 to 3
- spatial_qkv: bfloat16 [3, 2048, 2048], P(None, None, 'head')
- spatial_out: bfloat16 [2048, 2048], P('head'), may hold values from -0.125 to 0.125
- temporal_qkv: bfloat16 [3, 2048, 2048], P(None, None, 'head')
- temporal_out: bfloat16 [2048, 2048], P('head'), may hold values from -0.125 to 0.125
- hidden_weight: bfloat16 [2048, 8192], P(None, 'head'), may hold values from -0.125 to 0.125
- output_weight: bfloat16 [8192, 2048], P('head'), may hold values from -0.0625 to 0.0625
Outputs:
- block_out: bfloat16 [16, 1024, 2048], P(None, 'seq', 'head')
All inputs are finite; a program needn't handle non-finite values.
Results may differ from a plain program's by a relative error of at most 0.009.
Values may be sent and summed in bfloat16 or wider, within the bound.
A program may use at most 128 MiB of HBM per device.

v0:
```python
import jax
import jax.numpy as jnp
from jax import lax
from jax.sharding import PartitionSpec as P

HD = 64


def split_up(shard, dim, devices):
    lengths = shard.shape
    blocks = shard.reshape(*lengths[:dim], devices, lengths[dim] // devices, *lengths[dim + 1 :])
    return jnp.moveaxis(blocks, dim, 0)


def sum_at_owner(shard, axis, dim):
    devices = lax.axis_size(axis)
    blocks = lax.all_to_all(split_up(shard, dim, devices), axis, 0, 0, tiled=True)
    return jnp.sum(blocks.astype(jnp.float32), axis=0)


def layer_norm(values):
    average = jnp.mean(values, axis=-1, keepdims=True)
    centred = values - average
    variance = jnp.mean(centred * centred, axis=-1, keepdims=True)
    return centred * lax.rsqrt(variance + 1e-06)


def modulate(stream, modulation, offset):
    normed = layer_norm(stream.astype(jnp.float32))
    return (normed * (1.0 + modulation[offset + 1]) + modulation[offset]).astype(jnp.bfloat16)


def attend(query, keys, values):
    scores = jnp.einsum(
        "glhd,gmhd->ghlm", query, keys, preferred_element_type=jnp.float32
    ) * HD ** (-0.5)
    attn_weights = jax.nn.softmax(scores, axis=-1).astype(jnp.bfloat16)
    return jnp.einsum(
        "ghlm,gmhd->glhd", attn_weights, values, preferred_element_type=jnp.float32
    ).astype(jnp.bfloat16)


def project_three(normed, weights):
    return [
        jnp.dot(normed, weights[member], preferred_element_type=jnp.float32).astype(jnp.bfloat16)
        for member in range(3)
    ]


def column_adder(columns, portion):
    return jnp.dot(portion, columns, preferred_element_type=jnp.float32)


def per_device(
    latent,
    modulation,
    spatial_qkv,
    spatial_out,
    temporal_qkv,
    temporal_out,
    hidden_weight,
    output_weight,
):
    width_local = latent.shape[2]
    heads_local = width_local // HD
    anchor = lax.axis_index("head") * width_local
    local_rows = lax.dynamic_slice_in_dim(modulation, anchor, width_local, 1)
    full_spatial = lax.all_gather(latent, "head", axis=2, tiled=True)
    normed = modulate(full_spatial, modulation, 0)
    frames_local = latent.shape[0]
    patches = latent.shape[1]
    query, keys, values = [
        member.reshape(frames_local, patches, heads_local, HD)
        for member in project_three(normed, spatial_qkv)
    ]
    spatial = lax.map(
        lambda triple: attend(triple[0][None], triple[1][None], triple[2][None])[0],
        (query, keys, values),
    )
    spatial = spatial.reshape(frames_local, patches, width_local)
    columns = lax.all_to_all(spatial_out, "head", split_axis=1, concat_axis=0, tiled=True)
    reduced = column_adder(columns, lax.all_gather(spatial, "head", axis=2, tiled=True))
    stream_one = (latent.astype(jnp.float32) + local_rows[2] * reduced).astype(jnp.bfloat16)
    stream_temporal = lax.all_to_all(stream_one, "seq", split_axis=1, concat_axis=0, tiled=True)
    full_temporal = lax.all_gather(stream_temporal, "head", axis=2, tiled=True)
    normed = modulate(full_temporal, modulation, 3)
    query, keys, values = project_three(normed, temporal_qkv)
    frames = stream_temporal.shape[0]
    patches_local = stream_temporal.shape[1]

    def to_groups(tensor):
        return jnp.transpose(tensor.reshape(frames, patches_local, heads_local, HD), (1, 0, 2, 3))

    temporal = attend(to_groups(query), to_groups(keys), to_groups(values))
    temporal = jnp.transpose(temporal, (1, 0, 2, 3)).reshape(frames, patches_local, width_local)
    columns = lax.all_to_all(temporal_out, "head", split_axis=1, concat_axis=0, tiled=True)
    reduced = column_adder(columns, lax.all_gather(temporal, "head", axis=2, tiled=True))
    stream_two = (stream_temporal.astype(jnp.float32) + local_rows[5] * reduced).astype(
        jnp.bfloat16
    )
    full_two = lax.all_gather(stream_two, "head", axis=2, tiled=True)
    normed = modulate(full_two, modulation, 6)
    pre_act = jnp.dot(normed, hidden_weight, preferred_element_type=jnp.float32)
    hidden = jax.nn.gelu(pre_act, approximate=True).astype(jnp.bfloat16)
    partial_sums = jnp.dot(hidden, output_weight, preferred_element_type=jnp.float32)
    reduced = sum_at_owner(partial_sums.astype(jnp.bfloat16), "head", 2)
    return (stream_two.astype(jnp.float32) + local_rows[8] * reduced).astype(jnp.bfloat16)


def solution(mesh):
    in_specs = (
        P("seq", None, "head"),
        P(),
        P(None, None, "head"),
        P("head", None),
        P(None, None, "head"),
        P("head", None),
        P(None, "head"),
        P("head", None),
    )
    out_specs = P(None, "seq", "head")
    return jax.shard_map(
        per_device, mesh=mesh, in_specs=in_specs, out_specs=out_specs, check_vma=False
    )
```

profile of v0, /device:TPU:8, one launch (start us, length us, event | category | flops | bytes accessed | tf_op | source)
XLA Modules:
  0.0 685.8 jit_solution(7628114898617417352)
XLA Ops:
  8.4 99.1 %all-gather.6.cloned.1.call-done = bf16[1,1024,2048]{2,1,0:T(8,128)(2,1)} async-done(((bf16[1,1024,256]{2,1,0:T(8,128)(2,1)}), bf16[1,1024,2048]{2,1,0:T(8,128)(2,1)}) %all-gather.6.cloned.1.call-update) | async-done | bytes 4194320 | tf_op jit(solution)/shard_map/all_gather | solution.py:68
  107.6 3.0 convert_reduce_fusion.2
  112.3 1.9 fusion.33
  114.2 1.3 convolution_convert_fusion.6
  115.5 1.3 convolution_convert_fusion.5
  118.1 5.2 fusion.130
  123.3 8.1 %fusion.136 = f32[4,1024,1024]{1,2,0:T(8,128)} fusion(bf16[1024,4,64]{0,2,1:T(8,128)(2,1)S(1)} %bitcast.142, bf16[1024,4,64]{0,2,1:T(8,128)(2,1)S(1)} %bitcast.144), kind=kOutput, calls=%fused_computation.124 | convolution fusion | flops 536870912 | bytes 17825792 | tf_op jit(solution)/shard_map/while/body/eval_jaxpr/glhd,gmhd->ghlm/dot_general | solution.py:34
  131.4 16.0 %fusion.69 = bf16[4,64,1024]{2,1,0:T(8,128)(2,1)} fusion(bf16[1024,4,64]{0,2,1:T(8,128)(2,1)S(1)} %bitcast.162, f32[4,1024]{1,0:T(4,128)S(1)} %fusion.130, f32[4,1024,1024]{1,2,0:T(8,128)} %fusion.136), kind=kOutput, calls=%fused_computation.78 | convolution fusion | flops 558109696 | bytes 17842176 | tf_op jit(solution)/shard_map/while/body/eval_jaxpr/ghlm,gmhd->glhd/dot_general | solution.py:38
  147.4 1.3 copy.43
  148.7 6.0 all-to-all-start
  155.6 21.3 %all-to-all-done = bf16[256,8,256]{0,2,1:T(8,128)(2,1)S(1)} async-done(((bf16[256,8,256]{0,2,1:T(8,128)(2,1)}), bf16[256,8,256]{0,2,1:T(8,128)(2,1)S(1)}, u32[]{:S(2)}, u32[]{:S(2)}) %all-to-all-start) | async-done | bytes 1048608 | tf_op jit(solution)/shard_map/all_to_all | solution.py:81
  177.5 71.1 %all-gather.8.cloned.1.call-done = bf16[1,1024,2048]{1,2,0:T(8,128)(2,1)} async-done(((bf16[1,1024,256]{1,2,0:T(8,128)(2,1)}), bf16[1,1024,2048]{1,2,0:T(8,128)(2,1)}) %all-gather.8.cloned.1.call-update) | async-done | bytes 4194320 | tf_op jit(solution)/shard_map/all_gather | solution.py:82
  248.6 3.5 fusion.65
  253.4 3.8 reduce.6
  257.4 15.9 %all_to_all.55 = bf16[16,2,8192]{2,1,0:T(2,128)(2,1)S(1)} all-to-all(bf16[16,2,8192]{2,1,0:T(2,128)(2,1)S(1)} %reshape.181), channel_id=1, replica_groups=mesh['seq'=16,'head'=8] {'seq'}, dimensions={0} | all-to-all | bytes 1048576 | tf_op jit(solution)/shard_map/all_to_all | solution.py:84
  274.9 94.6 %all-gather.10.cloned.1.call-done = bf16[16,64,2048]{2,1,0:T(8,128)(2,1)} async-done(((bf16[16,64,256]{2,1,0:T(8,128)(2,1)}), bf16[16,64,2048]{2,1,0:T(8,128)(2,1)}) %all-gather.10.cloned.1.call-update) | async-done | bytes 4194320 | tf_op jit(solution)/shard_map/all_gather | solution.py:85
  369.5 3.0 convert_reduce_fusion.1
  374.2 3.0 convolution_convert_fusion.1
  377.5 4.2 convolution_convert_fusion.2
  382.2 5.0 convolution_convert_fusion.3
  387.2 2.2 reshape.170
  389.4 3.3 fusion.131
  392.7 2.5 fusion.54
  395.7 1.5 reshape.173
  397.4 24.8 %all_to_all.56 = bf16[256,8,256]{2,0,1:T(8,128)(2,1)S(1)} all-to-all(bf16[256,8,256]{2,0,1:T(8,128)(2,1)S(1)} %bitcast.138), channel_id=1, replica_groups=mesh['seq'=16,'head'=8] {'head'}, dimensions={1} | all-to-all | bytes 2097152 | tf_op jit(solution)/shard_map/all_to_all | solution.py:96
  422.2 74.8 %all-gather.12.cloned.1.call-done = bf16[16,64,2048]{2,1,0:T(8,128)(2,1)} async-done(((bf16[16,64,256]{2,1,0:T(8,128)(2,1)}), bf16[16,64,2048]{2,1,0:T(8,128)(2,1)}) %all-gather.12.cloned.1.call-update) | async-done | bytes 4194320 | tf_op jit(solution)/shard_map/all_gather | solution.py:97
  497.0 4.2 fusion.68
  501.3 100.4 %all-gather.14.cloned.1.call-done = bf16[16,64,2048]{2,1,0:T(8,128)(2,1)} async-done(((bf16[16,64,256]{2,1,0:T(8,128)(2,1)}), bf16[16,64,2048]{2,1,0:T(8,128)(2,1)}) %all-gather.14.cloned.1.call-update) | async-done | bytes 4194320 | tf_op jit(solution)/shard_map/all_gather | solution.py:101
  601.7 3.0 convert_reduce_fusion
  606.4 15.3 %fusion.45 = bf16[16,64,2048]{2,1,0:T(8,128)(2,1)} fusion(bf16[1024,2048]{1,0:T(8,128)(2,1)} %param.15, bf16[16,64,2048]{2,1,0:T(8,128)(2,1)} %all-gather.14.cloned.1.call-done, bf16[2048,1024]{1,0:T(8,128)(2,1)} %param.14, f32[2048]{0:T(1024)S(1)} %bitcast.152, f32[2048]{0:T(1024)S(1)} %bitcast.151, f32[16,64]{1,0:T(8,128)S(1)} %add_rsqrt_fusion, ...), kind=kOutput, calls=%fused_computation.54 | convolution fusion | flops 8614051840 | bytes 16801792 | tf_op jit(solution)/shard_map/dot_general | solution.py:105
  621.7 2.8 copy.89
  624.5 52.6 %all_to_all.57 = bf16[8,16,64,256]{3,2,1,0:T(8,128)(2,1)S(1)} all-to-all(bf16[8,16,64,256]{3,2,1,0:T(8,128)(2,1)S(1)} %bitcast.133), channel_id=1, replica_groups=mesh['seq'=16,'head'=8] {'head'}, dimensions={0} | all-to-all | bytes 8388608 | tf_op jit(solution)/shard_map/all_to_all | solution.py:17
  (52 shorter events, 16.3 us)
Async XLA Ops:
  6.5 101.0 %all-gather.6.cloned.1.call-start = ((), (), s32[]{:S(2)}) async-start(), calls=%async_computation.4 | async-start | bytes 4718592 | tf_op jit(solution)/shard_map/all_gather | solution.py:68
  7.3 241.3 %all-gather.8.cloned.1.call-start = ((), (), s32[]{:S(2)}) async-start(), calls=%async_computation.5 | async-start | bytes 4718592 | tf_op jit(solution)/shard_map/all_gather | solution.py:82
  107.6 3.4 copy-start
  112.3 1.9 copy-start.8
  131.4 16.0 %copy-start.5 = (bf16[256,2048]{1,0:T(8,128)(2,1)S(1)}, bf16[256,2048]{1,0:T(8,128)(2,1)}, u32[]{:S(2)}) copy-start(bf16[256,2048]{1,0:T(8,128)(2,1)} %param.11) | copy-start | bytes 3145732
  147.4 101.2 %copy-start.7 = (bf16[1,1024,256]{2,1,0:T(8,128)(2,1)S(1)}, bf16[1,1024,256]{2,1,0:T(8,128)(2,1)}, u32[]{:S(2)}) copy-start(bf16[1,1024,256]{2,1,0:T(8,128)(2,1)} %param.8) | copy-start | bytes 1572868
  148.7 28.2 %all-to-all-start = ((bf16[256,8,256]{0,2,1:T(8,128)(2,1)}), bf16[256,8,256]{0,2,1:T(8,128)(2,1)S(1)}, u32[]{:S(2)}, u32[]{:S(2)}) async-start(bf16[256,8,256]{0,2,1:T(8,128)(2,1)} %bitcast.14), calls=%async_computation | async-start | bytes 2097152 | tf_op jit(solution)/shard_map/all_to_all | solution.py:81
  154.7 214.7 %all-gather.10.cloned.1.call-start = ((), (), s32[]{:S(2)}) async-start(), calls=%async_computation.6 | async-start | bytes 4718592 | tf_op jit(solution)/shard_map/all_gather | solution.py:85
  274.7 222.4 %all-gather.12.cloned.1.call-start = ((), (), s32[]{:S(2)}) async-start(), calls=%async_computation.7 | async-start | bytes 4718592 | tf_op jit(solution)/shard_map/all_gather | solution.py:97
  369.5 3.4 copy-start.1
  395.2 2.1 copy-start.6
  395.2 101.8 %copy-start.3 = (bf16[1,1024,256]{2,1,0:T(8,128)(2,1)S(1)}, bf16[1,1024,256]{2,1,0:T(8,128)(2,1)}, u32[]{:S(2)}) copy-start(bf16[1,1024,256]{2,1,0:T(8,128)(2,1)} %copy.55) | copy-start | bytes 1572868
  397.2 204.5 %all-gather.14.cloned.1.call-start = ((), (), s32[]{:S(2)}) async-start(), calls=%async_computation.8 | async-start | bytes 4718592 | tf_op jit(solution)/shard_map/all_gather | solution.py:101
  601.7 3.4 copy-start.2
  677.1 1.0 copy-start.4
Sparse Core Ops, SparseCore 0:
  8.9 98.6 all-gather.5
  147.5 101.0 all-gather.7
  274.8 94.6 all-gather.9
  397.3 99.6 all-gather.11
  501.4 100.2 all-gather.13
where the time goes:
time: 696 us; the launch traced here: 686 us
  waiting for transfers between devices  462 us (66%)
  blocking collectives  93.3 us (13%)
  matrix products  74.2 us (11%)
  other arithmetic  21.1 us (3%)
  local copies, waits for them, and re-layouts  15.2 us (2%)
  between operations  13.6 us (2%)
    all_gather x1, waiting for transfers between devices, per_device(): full_two = lax.all_gather(stream_two, 'head', axis=2, tiled=True)  100 us
    all_gather x1, waiting for transfers between devices, per_device(): full_spatial = lax.all_gather(latent, 'head', axis=2, tiled=True)  99.1 us
    all_gather x1, waiting for transfers between devices, per_device(): full_temporal = lax.all_gather(stream_temporal, 'head', axis=2, tiled=True)  94.6 us
    all_gather x1, waiting for transfers between devices, per_device(): lax.all_gather(temporal, 'head', axis=2, tiled=True)  74.8 us
    all_gather x1, waiting for transfers between devices, per_device(): lax.all_gather(spatial, 'head', axis=2, tiled=True)  71.1 us
    all_to_all x1, blocking collectives, sum_at_owner(): lax.all_to_all(split_up(shard, dim, devices), axis, 0, 0, tiled=True)  52.6 us
    all_to_all x1, blocking collectives, per_device(): lax.all_to_all(temporal_out, 'head', split_axis=1, concat_axis=0, tiled=T...  24.8 us
    all_to_all x1, waiting for transfers between devices, per_device(): lax.all_to_all(spatial_out, 'head', split_axis=1, concat_axis=0, tiled=True)  21.3 us
  transfers between devices with their start and end apart: 6, of which 6 were waited for; matrix products, arithmetic and copies ran while one was open for 1% of the time, Pallas kernels for 0%

commit v1 on v0

--- a/solution.py
+++ b/solution.py
@@ -65,7 +65,9 @@
     heads_local = width_local // HD
     anchor = lax.axis_index("head") * width_local
     local_rows = lax.dynamic_slice_in_dim(modulation, anchor, width_local, 1)
-    full_spatial = lax.all_gather(latent, "head", axis=2, tiled=True)
+    p_next = jnp.stack([latent for _ in range(lax.axis_size("head"))])
+    all_rows = lax.all_to_all(p_next, "head", 0, 0)
+    full_spatial = jnp.concatenate(all_rows, 2)
     normed = modulate(full_spatial, modulation, 0)
     frames_local = latent.shape[0]
     patches = latent.shape[1]

time: 696 us -> 660 us (0.948)
  waiting for transfers between devices: 462 us -> 420 us
    all_gather x1 -> x0, waiting for transfers between devices: 99.1 us -> none  [per_device(): full_spatial = lax.all_gather(latent, 'head', axis=2, tiled=True)]
    all_to_all x0 -> x1, waiting for transfers between devices: none -> 58.4 us  [per_device(): all_rows = lax.all_to_all(p_next, 'head', 0, 0)]
where the time goes in v1:
time: 660 us; the launch traced here: 656 us
  waiting for transfers between devices  420 us (64%)
  blocking collectives  93.8 us (14%)
  matrix products  74.2 us (11%)
  other arithmetic  25.7 us (4%)
  local copies, waits for them, and re-layouts  18.9 us (3%)
  between operations  13.7 us (2%)
  starting transfers between devices  9.54 us (1%)
    all_gather x1, waiting for transfers between devices, per_device(): full_two = lax.all_gather(stream_two, 'head', axis=2, tiled=True)  100 us
    all_gather x1, waiting for transfers between devices, per_device(): full_temporal = lax.all_gather(stream_temporal, 'head', axis=2, tiled=True)  95.9 us
    all_gather x1, waiting for transfers between devices, per_device(): lax.all_gather(temporal, 'head', axis=2, tiled=True)  74.8 us
    all_gather x1, waiting for transfers between devices, per_device(): lax.all_gather(spatial, 'head', axis=2, tiled=True)  71.8 us
    all_to_all x1, waiting for transfers between devices, per_device(): all_rows = lax.all_to_all(p_next, 'head', 0, 0)  58.4 us
    all_to_all x1, blocking collectives, sum_at_owner(): lax.all_to_all(split_up(shard, dim, devices), axis, 0, 0, tiled=True)  52.6 us
    all_to_all x1, blocking collectives, per_device(): lax.all_to_all(temporal_out, 'head', split_axis=1, concat_axis=0, tiled=T...  24.9 us
    all_to_all x1, waiting for transfers between devices, per_device(): lax.all_to_all(spatial_out, 'head', split_axis=1, concat_axis=0, tiled=True)  19 us
  transfers between devices with their start and end apart: 6, of which 6 were waited for; matrix products, arithmetic and copies ran while one was open for 1% of the time, Pallas kernels for 0%

profile of v1, /device:TPU:8, one launch (start us, length us, event | category | flops | bytes accessed | tf_op | source)
XLA Modules:
  0.0 656.3 jit_solution(14974057974837063321)
XLA Ops:
  7.8 2.5 stack.2
  10.3 5.7 all-to-all-start
  17.2 58.4 %all-to-all-done = bf16[8,1,1024,256]{2,3,1,0:T(8,128)(2,1)} async-done(((bf16[8,1,1024,256]{2,3,1,0:T(8,128)(2,1)}), bf16[8,1,1024,256]{2,3,1,0:T(8,128)(2,1)}, u32[]{:S(2)}, u32[]{:S(2)}) %all-to-all-start) | async-done | bytes 4194336 | tf_op jit(solution)/shard_map/all_to_all | solution.py:69
  75.6 2.9 fusion.36
  78.4 3.2 bitcast_convert_fusion
  82.6 3.7 add_convert_fusion
  90.2 5.2 fusion.126
  95.5 8.1 %fusion.132 = f32[4,1024,1024]{1,2,0:T(8,128)} fusion(bf16[1024,4,64]{0,2,1:T(8,128)(2,1)S(1)} %bitcast.159, bf16[1024,4,64]{0,2,1:T(8,128)(2,1)S(1)} %bitcast.161), kind=kOutput, calls=%fused_computation.122 | convolution fusion | flops 536870912 | bytes 17825792 | tf_op jit(solution)/shard_map/while/body/eval_jaxpr/glhd,gmhd->ghlm/dot_general | solution.py:34
  103.5 16.0 %fusion.65 = bf16[4,64,1024]{2,1,0:T(8,128)(2,1)} fusion(bf16[1024,4,64]{0,2,1:T(8,128)(2,1)S(1)} %bitcast.178, f32[4,1024]{1,0:T(4,128)S(1)} %fusion.126, f32[4,1024,1024]{1,2,0:T(8,128)} %fusion.132), kind=kOutput, calls=%fused_computation.75 | convolution fusion | flops 558109696 | bytes 17842176 | tf_op jit(solution)/shard_map/while/body/eval_jaxpr/ghlm,gmhd->glhd/dot_general | solution.py:38
  120.9 3.6 all-to-all-start.1
  125.4 19.0 %all-to-all-done.1 = bf16[256,8,256]{0,2,1:T(8,128)(2,1)S(1)} async-done(((bf16[256,8,256]{0,2,1:T(8,128)(2,1)}), bf16[256,8,256]{0,2,1:T(8,128)(2,1)S(1)}, u32[]{:S(2)}, u32[]{:S(2)}) %all-to-all-start.1) | async-done | bytes 1048608 | tf_op jit(solution)/shard_map/all_to_all | solution.py:83
  145.4 71.8 %all-gather.5.cloned.1.call-done = bf16[1,1024,2048]{1,2,0:T(8,128)(2,1)} async-done(((bf16[1,1024,256]{1,2,0:T(8,128)(2,1)}), bf16[1,1024,2048]{1,2,0:T(8,128)(2,1)}) %all-gather.5.cloned.1.call-update) | async-done | bytes 4194320 | tf_op jit(solution)/shard_map/all_gather | solution.py:84
  217.2 3.5 fusion.61
  222.1 3.8 reduce.16
  226.0 16.4 %all_to_all.60 = bf16[16,2,8192]{2,1,0:T(2,128)(2,1)S(1)} all-to-all(bf16[16,2,8192]{2,1,0:T(2,128)(2,1)S(1)} %reshape.373), channel_id=1, replica_groups=mesh['seq'=16,'head'=8] {'seq'}, dimensions={0} | all-to-all | bytes 1048576 | tf_op jit(solution)/shard_map/all_to_all | solution.py:86
  244.0 95.9 %all-gather.7.cloned.1.call-done = bf16[16,64,2048]{2,1,0:T(8,128)(2,1)} async-done(((bf16[16,64,256]{2,1,0:T(8,128)(2,1)}), bf16[16,64,2048]{2,1,0:T(8,128)(2,1)}) %all-gather.7.cloned.1.call-update) | async-done | bytes 4194320 | tf_op jit(solution)/shard_map/all_gather | solution.py:87
  340.0 3.0 convert_reduce_fusion.1
  344.7 3.0 convolution_convert_fusion.1
  348.0 4.2 convolution_convert_fusion.2
  352.7 5.0 convolution_convert_fusion.3
  357.7 2.2 reshape.349
  359.9 3.3 fusion.127
  363.2 2.5 fusion.50
  366.2 1.5 reshape.352
  367.8 24.9 %all_to_all.61 = bf16[256,8,256]{2,0,1:T(8,128)(2,1)S(1)} all-to-all(bf16[256,8,256]{2,0,1:T(8,128)(2,1)S(1)} %bitcast.155), channel_id=1, replica_groups=mesh['seq'=16,'head'=8] {'head'}, dimensions={1} | all-to-all | bytes 2097152 | tf_op jit(solution)/shard_map/all_to_all | solution.py:98
  392.7 74.8 %all-gather.9.cloned.1.call-done = bf16[16,64,2048]{2,1,0:T(8,128)(2,1)} async-done(((bf16[16,64,256]{2,1,0:T(8,128)(2,1)}), bf16[16,64,2048]{2,1,0:T(8,128)(2,1)}) %all-gather.9.cloned.1.call-update) | async-done | bytes 4194320 | tf_op jit(solution)/shard_map/all_gather | solution.py:99
  467.5 4.2 fusion.64
  471.8 100.4 %all-gather.11.cloned.1.call-done = bf16[16,64,2048]{2,1,0:T(8,128)(2,1)} async-done(((bf16[16,64,256]{2,1,0:T(8,128)(2,1)}), bf16[16,64,2048]{2,1,0:T(8,128)(2,1)}) %all-gather.11.cloned.1.call-update) | async-done | bytes 4194320 | tf_op jit(solution)/shard_map/all_gather | solution.py:103
  572.2 3.0 convert_reduce_fusion
  576.9 15.3 %fusion.41 = bf16[16,64,2048]{2,1,0:T(8,128)(2,1)} fusion(bf16[1024,2048]{1,0:T(8,128)(2,1)} %param.15, bf16[16,64,2048]{2,1,0:T(8,128)(2,1)} %all-gather.11.cloned.1.call-done, bf16[2048,1024]{1,0:T(8,128)(2,1)} %param.14, f32[2048]{0:T(1024)S(1)} %bitcast.168, f32[2048]{0:T(1024)S(1)} %bitcast.167, f32[16,64]{1,0:T(8,128)S(1)} %add_rsqrt_fusion, ...), kind=kOutput, calls=%fused_computation.51 | convolution fusion | flops 8614051840 | bytes 16801792 | tf_op jit(solution)/shard_map/dot_general | solution.py:107
  592.2 2.8 copy.95
  595.0 52.6 %all_to_all.62 = bf16[8,16,64,256]{3,2,1,0:T(8,128)(2,1)S(1)} all-to-all(bf16[8,16,64,256]{3,2,1,0:T(8,128)(2,1)S(1)} %bitcast.147), channel_id=1, replica_groups=mesh['seq'=16,'head'=8] {'head'}, dimensions={0} | all-to-all | bytes 8388608 | tf_op jit(solution)/shard_map/all_to_all | solution.py:17
  (54 shorter events, 20.6 us)
Async XLA Ops:
  10.3 65.3 %all-to-all-start = ((bf16[8,1,1024,256]{2,3,1,0:T(8,128)(2,1)}), bf16[8,1,1024,256]{2,3,1,0:T(8,128)(2,1)}, u32[]{:S(2)}, u32[]{:S(2)}) async-start(bf16[8,1,1024,256]{2,3,1,0:T(8,128)(2,1)} %stack.2), calls=%async_computation | async-start | bytes 8388608 | tf_op jit(solution)/shard_map/all_to_all | solution.py:69
  15.9 201.3 %all-gather.5.cloned.1.call-start = ((), (), s32[]{:S(2)}) async-start(), calls=%async_computation.5 | async-start | bytes 4718592 | tf_op jit(solution)/shard_map/all_gather | solution.py:84
  82.6 3.7 copy-start.7
  103.5 16.0 %copy-start.4 = (bf16[256,2048]{1,0:T(8,128)(2,1)S(1)}, bf16[256,2048]{1,0:T(8,128)(2,1)}, u32[]{:S(2)}) copy-start(bf16[256,2048]{1,0:T(8,128)(2,1)} %param.11) | copy-start | bytes 3145732
  119.5 97.7 %copy-start.6 = (bf16[1,1024,256]{2,1,0:T(8,128)(2,1)S(1)}, bf16[1,1024,256]{2,1,0:T(8,128)(2,1)}, u32[]{:S(2)}) copy-start(bf16[1,1024,256]{2,1,0:T(8,128)(2,1)} %param.8) | copy-start | bytes 1572868
  120.9 23.5 %all-to-all-start.1 = ((bf16[256,8,256]{0,2,1:T(8,128)(2,1)}), bf16[256,8,256]{0,2,1:T(8,128)(2,1)S(1)}, u32[]{:S(2)}, u32[]{:S(2)}) async-start(bf16[256,8,256]{0,2,1:T(8,128)(2,1)} %bitcast.18), calls=%async_computation.1 | async-start | bytes 2097152 | tf_op jit(solution)/shard_map/all_to_all | solution.py:83
  124.5 215.5 %all-gather.7.cloned.1.call-start = ((), (), s32[]{:S(2)}) async-start(), calls=%async_computation.6 | async-start | bytes 4718592 | tf_op jit(solution)/shard_map/all_gather | solution.py:87
  243.8 223.7 %all-gather.9.cloned.1.call-start = ((), (), s32[]{:S(2)}) async-start(), calls=%async_computation.7 | async-start | bytes 4718592 | tf_op jit(solution)/shard_map/all_gather | solution.py:99
  340.0 3.4 copy-start
  365.7 2.1 copy-start.5
  365.7 101.8 %copy-start.2 = (bf16[1,1024,256]{2,1,0:T(8,128)(2,1)S(1)}, bf16[1,1024,256]{2,1,0:T(8,128)(2,1)}, u32[]{:S(2)}) copy-start(bf16[1,1024,256]{2,1,0:T(8,128)(2,1)} %copy.61) | copy-start | bytes 1572868
  367.7 204.5 %all-gather.11.cloned.1.call-start = ((), (), s32[]{:S(2)}) async-start(), calls=%async_computation.8 | async-start | bytes 4718592 | tf_op jit(solution)/shard_map/all_gather | solution.py:103
  572.2 3.4 copy-start.1
  647.5 1.0 copy-start.3
Sparse Core Ops, SparseCore 0:
  119.7 97.5 all-gather.4
  243.9 95.9 all-gather.6
  367.8 99.6 all-gather.8
  471.9 100.2 all-gather.10
